TPU v7x, 32 devices: a whole 2x2x4 slice. The times are simulated.
32 devices in a mesh: row: 2 (over x), col: 4 (over y, core), layer: 4 (over z).
Axes of the slice: x: 2, y: 2, z: 4, core: 2. Of those that a mesh axis runs over, the one named last changes fastest.
Arguments:
- panel: float32 [1024, 8192], P('layer', ('col', 'row')), may hold values from -0.75 to 0.75
- c_in: float32 [4, 2, 1024, 8192], P('layer', 'row', None, 'col'), may hold values from -1.5 to 1.5
Outputs:
- updated: float32 [4, 2, 1024, 8192], P('layer', 'row', None, 'col')
All inputs are finite; a program needn't handle non-finite values.
Results may differ from a plain program's by a relative error of at most 0.000062.
Values sent between devices are 32-bit elements; how exact they have to be, the bound alone decides.
A program may use at most 128 MiB of HBM per device.

v0:
```python
import jax
import jax.numpy as jnp
from jax import lax
from jax.sharding import PartitionSpec as P


def product(left, right):
    return lax.dot_general(
        left,
        right,
        (((0,), (0,)), ((), ())),
        precision=lax.Precision.HIGHEST,
        preferred_element_type=jnp.float32,
    )


def on_device(panel, c_in):
    narrow = c_in.shape[2]
    spread = lax.all_gather(panel, "col", axis=1, tiled=True)
    local = lax.all_gather(panel, "row", axis=1, tiled=True)
    pairs = (spread, local)
    groups = pairs[0].shape[1] // narrow
    columns_here = pairs[1].shape[1]
    spread, local = pairs
    tile = product(spread, local)
    tile = tile.reshape(groups, 1, narrow, columns_here)
    summed = lax.psum_scatter(tile, "layer", scatter_dimension=0, tiled=True)
    return c_in + summed


def solution(mesh):
    placed = (P("layer", ("col", "row")), P("layer", "row", None, "col"))
    return jax.shard_map(
        on_device,
        mesh=mesh,
        in_specs=placed,
        out_specs=P("layer", "row", None, "col"),
        check_vma=False,
    )
```

profile of v0, /device:TPU:0, one launch (start us, length us, event | category | flops | bytes accessed | tf_op | source)
XLA Modules:
  0.0 683.8 jit_solution(14845366187475919267)
XLA Ops:
  6.5 0.0 all-gather.5.cloned.1.call-start
  6.5 0.7 all-gather.5.cloned.1.call-update
  7.3 0.0 all-gather.3.cloned.1.call-start
  7.3 0.7 all-gather.3.cloned.1.call-update
  8.0 0.0 reduce-scatter.2.cloned.1.call-start
  8.1 36.7 %all-gather.5.cloned.1.call-done = f32[256,2048]{1,0:T(8,128)} async-done(((f32[256,1024]{1,0:T(8,128)}), f32[256,2048]{1,0:T(8,128)}) %all-gather.5.cloned.1.call-update) | async-done | bytes 2097168 | tf_op jit(solution)/shard_map/all_gather | solution.py:20
  44.7 36.1 %all-gather.3.cloned.1.call-done = f32[256,4096]{1,0:T(8,128)} async-done(((f32[256,1024]{1,0:T(8,128)}), f32[256,4096]{1,0:T(8,128)}) %all-gather.3.cloned.1.call-update) | async-done | bytes 4194320 | tf_op jit(solution)/shard_map/all_gather | solution.py:19
  80.8 32.3 %fusion = f32[4096,2048]{1,0:T(8,128)} fusion(f32[256,4096]{1,0:T(8,128)} %all-gather.3.cloned.1.call-done, f32[256,2048]{1,0:T(8,128)} %all-gather.5.cloned.1.call-done), kind=kOutput, calls=%fused_computation | convolution fusion | flops 25769803776 | bytes 39845888 | tf_op jit(solution)/shard_map/dot_general | solution.py:8
  113.1 0.0 reduce-scatter.2.cloned.1.call-update
  113.1 552.3 %reduce-scatter.2.cloned.1.call-done = f32[1,1,1024,2048]{3,2,1,0:T(8,128)} async-done(((f32[4,1,1024,2048]{3,2,1,0:T(8,128)}), f32[1,1,1024,2048]{3,2,1,0:T(8,128)}) %reduce-scatter.2.cloned.1.call-update) | async-done | bytes 8388624 | tf_op jit(solution)/shard_map/reduce_scatter | solution.py:27
  665.4 11.9 %add.5 = f32[1,1,1024,2048]{3,2,1,0:T(8,128)} add(f32[1,1,1024,2048]{3,2,1,0:T(8,128)} %param.3, f32[1,1,1024,2048]{3,2,1,0:T(8,128)} %reduce-scatter.2.cloned.1.call-done) | non-fusion elementwise | flops 2097152 | bytes 25165824 | tf_op jit(solution)/shard_map/add | solution.py:28
Async XLA Ops:
  6.5 38.2 %all-gather.5.cloned.1.call-start = ((), (), s32[]{:S(2)}) async-start(), calls=%async_computation.2 | async-start | bytes 3145728 | tf_op jit(solution)/shard_map/all_gather | solution.py:20
  7.3 73.5 %all-gather.3.cloned.1.call-start = ((), (), s32[]{:S(2)}) async-start(), calls=%async_computation.1 | async-start | bytes 5242880 | tf_op jit(solution)/shard_map/all_gather | solution.py:19
  8.0 657.4 %reduce-scatter.2.cloned.1.call-start = ((), (), s32[]{:S(2)}) async-start(), calls=%async_computation.3 | async-start | bytes 41943040 | tf_op jit(solution)/shard_map/reduce_scatter | solution.py:27
Sparse Core Ops, SparseCore 0:
  8.9 35.8 all-gather.4
  46.3 34.4 all-gather.2
  113.2 552.1 reduce-scatter.1
where the time goes:
time: 684 us
  waiting for transfers between devices  626 us (92%)
  matrix products  32.3 us (5%)
  between operations  13.1 us (2%)
  other arithmetic  11.9 us (2%)
    reduce_scatter x1, waiting for transfers between devices, on_device(): summed = lax.psum_scatter(tile, 'layer', scatter_dimension=0, tiled=True)  552 us
    all_gather x1, waiting for transfers between devices, on_device(): local = lax.all_gather(panel, 'row', axis=1, tiled=True)  36.7 us
    all_gather x1, waiting for transfers between devices, on_device(): spread = lax.all_gather(panel, 'col', axis=1, tiled=True)  36.1 us
    dot_general x1, matrix products, product(): lax.dot_general(left, right, (((0,), (0,)), ((), ())), precision=lax.Prec...  32.3 us
  transfers between devices with their start and end apart: 3, of which 3 were waited for; matrix products, arithmetic and copies ran while one was open for 0% of the time, Pallas kernels for 0%

commit v1 on v0

v1 whole, which is shorter than its diff:
```python
import functools

import jax
import jax.numpy as jnp
from jax import lax
from jax.experimental import pallas as pl
from jax.experimental.pallas import tpu as pltpu
from jax.sharding import PartitionSpec as P

MESH = pl.DeviceIdType.MESH


def product(left, right):
    return lax.dot_general(
        left,
        right,
        (((0,), (0,)), ((), ())),
        precision=lax.Precision.HIGHEST,
        preferred_element_type=jnp.float32,
    )


def general(panel, c_in):
    narrow = c_in.shape[2]
    spread = lax.all_gather(panel, "col", axis=1, tiled=True)
    local = lax.all_gather(panel, "row", axis=1, tiled=True)
    groups = spread.shape[1] // narrow
    tile = product(spread, local)
    tile = tile.reshape(groups, 1, narrow, local.shape[1])
    summed = lax.psum_scatter(tile, "layer", scatter_dimension=0, tiled=True)
    return c_in + summed


def gather_and_update(
    panel, c_in, out, cols, rows, left3, own_sem, c_sem,
    got, row_got, to_x, to_in, to_out, to_partner, to_far,
):
    x = lax.axis_index("row")
    c = lax.axis_index("col")
    z = lax.axis_index("layer")
    depth, narrow = panel.shape
    half = depth // 2
    flip = z // 2
    lane = c % 2
    inward = z + 1 - 2 * flip
    outward = z - 1 + 2 * flip
    at_end = (z == 0) | (z == 3)
    partner = c + 1 - 2 * lane
    far = 2 * (1 - flip)
    is_owner = c == z
    is_far = (c // 2) != flip
    same, other = x, 1 - x

    def layer(k):
        return k + flip * (3 - 2 * k)

    def part(h):
        return pl.ds(pl.multiple_of(h * half, half), half)

    def remote(src, dst, send_sem, recv_sem, **device):
        return pltpu.make_async_remote_copy(
            src_ref=src, dst_ref=dst, send_sem=send_sem, recv_sem=recv_sem,
            device_id=device, device_id_type=MESH,
        )

    def chunk_copy(b, k, h, sems, **device):
        ref = cols.at[b, layer(k), part(h)]
        return remote(ref, ref, sems.at[b, layer(k), h], got.at[b, layer(k), h], **device)

    def arrived(b, k, h):
        chunk_copy(b, k, h, to_x, row=1 - x).wait_recv()

    def row_arrived(k, h):
        ref = rows.at[layer(k), part(h)]
        remote(ref, ref, to_partner.at[layer(k), h], row_got.at[layer(k), h], col=partner).wait_recv()

    def owner_copies(k, h):
        src = cols.at[same, layer(k), part(h)]
        dst = rows.at[layer(k), part(h)]
        return (
            remote(src, dst, to_far.at[layer(k), h], row_got.at[layer(k), h], col=far + h),
            remote(src, dst, to_partner.at[layer(k), h], row_got.at[layer(k), h], col=partner),
        )

    def far_copy(k):
        ref = rows.at[layer(k), part(lane)]
        return remote(ref, ref, to_partner.at[layer(k), lane], row_got.at[layer(k), lane], col=partner)

    def share_rows(k, h):
        @pl.when(is_owner)
        def _():
            for copy in owner_copies(k, h):
                copy.start()

    def prepare(k):
        @pl.when(is_far)
        def _():
            row_arrived(k, lane)
            far_copy(k).start()
            row_arrived(k, 1 - lane)

        @pl.when(jnp.logical_not(is_far) & jnp.logical_not(is_owner))
        def _():
            row_arrived(k, 0)
            row_arrived(k, 1)

        def split(load):
            def body(i, carry):
                span = pl.ds(pl.multiple_of(i * 256, 256), 256)
                block = load(span).T
                high = block.astype(jnp.bfloat16)
                low = (block - high.astype(jnp.float32)).astype(jnp.bfloat16)
                left3[span, 0:depth] = high
                left3[span, depth : 2 * depth] = high
                left3[span, 2 * depth : 3 * depth] = low
                return carry

            lax.fori_loop(0, narrow // 256, body, 0)

        @pl.when(is_owner)
        def _():
            split(lambda span: cols[same, layer(k), :, span])

        @pl.when(jnp.logical_not(is_owner))
        def _():
            split(lambda span: rows[layer(k), :, span])

    def multiply(b, k):
        def body(i, carry):
            span = pl.ds(pl.multiple_of(i * 256, 256), 256)
            wide = pl.ds(pl.multiple_of(b * narrow + i * 256, 256), 256)
            block = cols[b, layer(k), :, span]
            high = block.astype(jnp.bfloat16)
            low = (block - high.astype(jnp.float32)).astype(jnp.bfloat16)
            right3 = jnp.concatenate([high, low, high], axis=0)
            for m in range(0, narrow, 512):
                out[m : m + 512, wide] += jnp.dot(
                    left3[m : m + 512, :], right3, preferred_element_type=jnp.float32
                )
            return carry

        lax.fori_loop(0, narrow // 256, body, 0)

    own = pltpu.make_async_copy(panel, cols.at[same, z], own_sem)
    own.start()
    base = pltpu.make_async_copy(c_in, out, c_sem)
    base.start()

    barrier = pltpu.get_barrier_semaphore()

    def greet(**device):
        pl.semaphore_signal(barrier, inc=1, device_id=device, device_id_type=MESH)

    greet(row=1 - x)
    greet(layer=inward)
    for step in range(1, 4):
        greet(col=(c + step) % 4)

    @pl.when(jnp.logical_not(at_end))
    def _():
        greet(layer=outward)

    pl.semaphore_wait(barrier, jnp.where(at_end, 5, 6))
    own.wait()

    @pl.when(at_end)
    def _():
        sent = []

        def send(b, k, h, sems, **device):
            copy = chunk_copy(b, k, h, sems, **device)
            copy.start()
            sent.append(copy)

        for h in range(2):
            send(same, 0, h, to_in, layer=inward)
            send(same, 0, h, to_x, row=1 - x)
            share_rows(0, h)
        for h in range(2):
            arrived(same, 1, h)
            send(same, 1, h, to_x, row=1 - x)
            share_rows(1, h)
            arrived(other, 0, h)
            send(other, 0, h, to_in, layer=inward)
        base.wait()
        prepare(0)
        multiply(same, 0)
        multiply(other, 0)
        arrived(same, 2, 0)
        send(same, 2, 0, to_x, row=1 - x)
        share_rows(2, 0)
        prepare(1)
        multiply(same, 1)
        arrived(same, 2, 1)
        send(same, 2, 1, to_x, row=1 - x)
        share_rows(2, 1)
        arrived(other, 1, 0)
        arrived(other, 1, 1)
        multiply(other, 1)
        arrived(same, 3, 0)
        send(same, 3, 0, to_x, row=1 - x)
        share_rows(3, 0)
        prepare(2)
        multiply(same, 2)
        arrived(same, 3, 1)
        share_rows(3, 1)
        arrived(other, 2, 0)
        arrived(other, 2, 1)
        multiply(other, 2)
        prepare(3)
        multiply(same, 3)
        arrived(other, 3, 0)
        arrived(other, 3, 1)
        multiply(other, 3)
        for copy in sent:
            copy.wait_send()

    @pl.when(jnp.logical_not(at_end))
    def _():
        sent = []

        def send(b, k, h, sems, **device):
            copy = chunk_copy(b, k, h, sems, **device)
            copy.start()
            sent.append(copy)

        for h in range(2):
            send(same, 1, h, to_out, layer=outward)
            send(same, 1, h, to_in, layer=inward)
            send(same, 1, h, to_x, row=1 - x)
            share_rows(1, h)
        for h in range(2):
            arrived(same, 2, h)
            send(same, 2, h, to_out, layer=outward)
            send(same, 2, h, to_x, row=1 - x)
            share_rows(2, h)
            arrived(same, 0, h)
            send(same, 0, h, to_in, layer=inward)
            share_rows(0, h)
        base.wait()
        prepare(1)
        multiply(same, 1)
        arrived(other, 1, 0)
        arrived(other, 1, 1)
        multiply(other, 1)
        for h in range(2):
            arrived(same, 3, h)
            send(same, 3, h, to_out, layer=outward)
            send(same, 3, h, to_x, row=1 - x)
            share_rows(3, h)
        prepare(0)
        multiply(same, 0)
        arrived(other, 0, 0)
        arrived(other, 0, 1)
        multiply(other, 0)
        prepare(2)
        multiply(same, 2)
        arrived(other, 2, 0)
        arrived(other, 2, 1)
        arrived(other, 3, 0)
        arrived(other, 3, 1)
        send(other, 3, 1, to_out, layer=outward)
        multiply(other, 2)
        prepare(3)
        multiply(same, 3)
        multiply(other, 3)
        for copy in sent:
            copy.wait_send()

    @pl.when(is_owner)
    def _():
        for k in range(4):
            for h in range(2):
                for copy in owner_copies(k, h):
                    copy.wait_send()

    @pl.when(is_far)
    def _():
        for k in range(4):
            far_copy(k).wait_send()


def lined_up(panel, c_in):
    depth, narrow = panel.shape
    wide = c_in.shape[3]
    dma = pltpu.SemaphoreType.DMA
    updated = pl.pallas_call(
        gather_and_update,
        out_shape=pltpu.VMEM((narrow, wide), jnp.float32),
        in_specs=[pl.BlockSpec(memory_space=pl.ANY)] * 2,
        out_specs=pl.BlockSpec(memory_space=pltpu.VMEM),
        scratch_shapes=[
            pltpu.VMEM((2, 4, depth, narrow), jnp.float32),
            pltpu.VMEM((4, depth, narrow), jnp.float32),
            pltpu.VMEM((narrow, 3 * depth), jnp.bfloat16),
            dma, dma,
            dma((2, 4, 2)),
            dma((4, 2)),
            dma((2, 4, 2)),
            dma((2, 4, 2)),
            dma((2, 4, 2)),
            dma((4, 2)),
            dma((4, 2)),
        ],
        compiler_params=pltpu.CompilerParams(
            collective_id=0, has_side_effects=True, vmem_limit_bytes=48 << 20
        ),
    )(panel, c_in.reshape(narrow, wide))
    return updated.reshape(c_in.shape)


def on_device(sizes, panel, c_in):
    depth, narrow = panel.shape
    fits = (
        sizes == (2, 4, 4)
        and c_in.shape == (1, 1, narrow, 2 * narrow)
        and narrow % 512 == 0
        and depth % 256 == 0
    )
    return (lined_up if fits else general)(panel, c_in)


def solution(mesh):
    sizes = tuple(mesh.shape[name] for name in ("row", "col", "layer"))
    return jax.shard_map(
        functools.partial(on_device, sizes),
        mesh=mesh,
        in_specs=(P("layer", ("col", "row")), P("layer", "row", None, "col")),
        out_specs=P("layer", "row", None, "col"),
        check_vma=False,
    )
```

time: 684 us -> 94.3 us (0.14)
  waiting for transfers between devices: 626 us -> 0 us
  Pallas kernels: 0 us -> 90.8 us
  matrix products: 32.3 us -> 0 us
  between operations: 13.1 us -> 0.01 us
  other arithmetic: 11.9 us -> 0 us
    reduce_scatter x1 -> x0, waiting for transfers between devices: 552 us -> none  [on_device(): summed = lax.psum_scatter(tile, 'layer', scatter_dimension=0, tiled=True)]
    pallas_call x0 -> x1, Pallas kernels: none -> 90.8 us  [lined_up(): pl.pallas_call(gather_and_update, out_shape=pltpu.VMEM((narrow, wide), jn...]
    all_gather x2 -> x0, waiting for transfers between devices: 72.7 us -> none  [the longest x1 36.7 us: on_device(): local = lax.all_gather(panel, 'row', axis=1, tiled=True)]
    dot_general x1 -> x0, matrix products: 32.3 us -> none  [product(): lax.dot_general(left, right, (((0,), (0,)), ((), ())), precision=lax.Prec...]
    add x1 -> x0, other arithmetic: 11.9 us -> none  [on_device(): return c_in + summed]
  transfers between devices with their start and end apart: 3 -> 0, of which waited for: 3 -> 0; matrix products, arithmetic and copies ran while one was open for 0% -> 0% of each run, Pallas kernels for 0% -> 0%
where the time goes in v1:
time: 94.3 us; the launch traced here: 94.2 us
  Pallas kernels  90.8 us (96%)
  local copies, waits for them, and re-layouts  3.4 us (4%)
    pallas_call x1, Pallas kernels, lined_up(): pl.pallas_call(gather_and_update, out_shape=pltpu.VMEM((narrow, wide), jn...  90.8 us
    unnamed x1, local copies, waits for them, and re-layouts  3.4 us

profile of v1, /device:TPU:0, one launch (start us, length us, event | category | flops | bytes accessed | tf_op | source)
XLA Modules:
  0.0 94.2 jit_solution(1255272313499817949)
XLA Ops:
  0.0 90.8 %shard_map.28 = f32[1024,2048]{1,0:T(8,128)S(1)} custom-call(f32[256,1024]{1,0:T(8,128)} %panel.1, f32[1024,2048]{1,0:T(8,128)} %bitcast.3), custom_call_target="tpu_custom_call" | custom-call | tf_op jit(solution)/shard_map/pallas_call | solution.py:287
  90.8 3.4 %copy.4 = f32[1,1,1024,2048]{3,2,1,0:T(8,128)} copy(f32[1,1,1024,2048]{3,2,1,0:T(8,128)S(1)} %bitcast.2) | data formatting | bytes 16777216

commit v2 on v1

--- a/solution.py
+++ b/solution.py
@@ -39,7 +39,7 @@
     c = lax.axis_index("col")
     z = lax.axis_index("layer")
     depth, narrow = panel.shape
-    half = depth // 2
+    width = narrow // 4
     flip = z // 2
     lane = c % 2
     inward = z + 1 - 2 * flip
@@ -55,7 +55,7 @@
         return k + flip * (3 - 2 * k)
 
     def part(h):
-        return pl.ds(pl.multiple_of(h * half, half), half)
+        return pl.ds(pl.multiple_of(h * width, width), width)
 
     def remote(src, dst, send_sem, recv_sem, **device):
         return pltpu.make_async_remote_copy(
@@ -64,27 +64,27 @@
         )
 
     def chunk_copy(b, k, h, sems, **device):
-        ref = cols.at[b, layer(k), part(h)]
+        ref = cols.at[b, layer(k), :, part(h)]
         return remote(ref, ref, sems.at[b, layer(k), h], got.at[b, layer(k), h], **device)
 
     def arrived(b, k, h):
         chunk_copy(b, k, h, to_x, row=1 - x).wait_recv()
 
     def row_arrived(k, h):
-        ref = rows.at[layer(k), part(h)]
+        ref = rows.at[layer(k), :, part(h)]
         remote(ref, ref, to_partner.at[layer(k), h], row_got.at[layer(k), h], col=partner).wait_recv()
 
     def owner_copies(k, h):
-        src = cols.at[same, layer(k), part(h)]
-        dst = rows.at[layer(k), part(h)]
+        src = cols.at[same, layer(k), :, part(h)]
+        dst = rows.at[layer(k), :, part(h)]
         return (
-            remote(src, dst, to_far.at[layer(k), h], row_got.at[layer(k), h], col=far + h),
+            remote(src, dst, to_far.at[layer(k), h], row_got.at[layer(k), h], col=far + h % 2),
             remote(src, dst, to_partner.at[layer(k), h], row_got.at[layer(k), h], col=partner),
         )
 
-    def far_copy(k):
-        ref = rows.at[layer(k), part(lane)]
-        return remote(ref, ref, to_partner.at[layer(k), lane], row_got.at[layer(k), lane], col=partner)
+    def far_copy(k, h):
+        ref = rows.at[layer(k), :, part(h)]
+        return remote(ref, ref, to_partner.at[layer(k), h], row_got.at[layer(k), h], col=partner)
 
     def share_rows(k, h):
         @pl.when(is_owner)
@@ -95,18 +95,20 @@
     def prepare(k):
         @pl.when(is_far)
         def _():
-            row_arrived(k, lane)
-            far_copy(k).start()
-            row_arrived(k, 1 - lane)
+            for h in (lane, lane + 2):
+                row_arrived(k, h)
+                far_copy(k, h).start()
+            for h in (1 - lane, 3 - lane):
+                row_arrived(k, h)
 
         @pl.when(jnp.logical_not(is_far) & jnp.logical_not(is_owner))
         def _():
-            row_arrived(k, 0)
-            row_arrived(k, 1)
+            for h in range(4):
+                row_arrived(k, h)
 
         def split(load):
             def body(i, carry):
-                span = pl.ds(pl.multiple_of(i * 256, 256), 256)
+                span = part(i)
                 block = load(span).T
                 high = block.astype(jnp.bfloat16)
                 low = (block - high.astype(jnp.float32)).astype(jnp.bfloat16)
@@ -115,7 +117,7 @@
                 left3[span, 2 * depth : 3 * depth] = low
                 return carry
 
-            lax.fori_loop(0, narrow // 256, body, 0)
+            lax.fori_loop(0, 4, body, 0)
 
         @pl.when(is_owner)
         def _():
@@ -125,10 +127,10 @@
         def _():
             split(lambda span: rows[layer(k), :, span])
 
-    def multiply(b, k):
+    def multiply(b, k, first=0, step=1):
         def body(i, carry):
-            span = pl.ds(pl.multiple_of(i * 256, 256), 256)
-            wide = pl.ds(pl.multiple_of(b * narrow + i * 256, 256), 256)
+            span = part(first + i * step)
+            wide = pl.ds(pl.multiple_of(b * narrow + (first + i * step) * width, width), width)
             block = cols[b, layer(k), :, span]
             high = block.astype(jnp.bfloat16)
             low = (block - high.astype(jnp.float32)).astype(jnp.bfloat16)
@@ -139,7 +141,7 @@
                 )
             return carry
 
-        lax.fori_loop(0, narrow // 256, body, 0)
+        lax.fori_loop(0, 4 // step, body, 0)
 
     own = pltpu.make_async_copy(panel, cols.at[same, z], own_sem)
     own.start()
@@ -172,11 +174,16 @@
             copy.start()
             sent.append(copy)
 
-        for h in range(2):
+        def relay(k, h):
+            arrived(same, k, h)
+            send(same, k, h, to_x, row=1 - x)
+            share_rows(k, h)
+
+        for h in range(4):
             send(same, 0, h, to_in, layer=inward)
             send(same, 0, h, to_x, row=1 - x)
             share_rows(0, h)
-        for h in range(2):
+        for h in range(4):
             arrived(same, 1, h)
             send(same, 1, h, to_x, row=1 - x)
             share_rows(1, h)
@@ -186,32 +193,31 @@
         prepare(0)
         multiply(same, 0)
         multiply(other, 0)
-        arrived(same, 2, 0)
-        send(same, 2, 0, to_x, row=1 - x)
-        share_rows(2, 0)
+        for h in (0, 1):
+            relay(2, h)
         prepare(1)
         multiply(same, 1)
-        arrived(same, 2, 1)
-        send(same, 2, 1, to_x, row=1 - x)
-        share_rows(2, 1)
-        arrived(other, 1, 0)
-        arrived(other, 1, 1)
+        for h in (2, 3):
+            relay(2, h)
+        for h in range(4):
+            arrived(other, 1, h)
         multiply(other, 1)
-        arrived(same, 3, 0)
-        send(same, 3, 0, to_x, row=1 - x)
-        share_rows(3, 0)
+        for h in (0, 1):
+            relay(3, h)
         prepare(2)
         multiply(same, 2)
-        arrived(same, 3, 1)
-        share_rows(3, 1)
-        arrived(other, 2, 0)
-        arrived(other, 2, 1)
+        for h in (2, 3):
+            arrived(same, 3, h)
+            share_rows(3, h)
+        for h in range(4):
+            arrived(other, 2, h)
         multiply(other, 2)
         prepare(3)
         multiply(same, 3)
-        arrived(other, 3, 0)
-        arrived(other, 3, 1)
-        multiply(other, 3)
+        for first in (0, 1):
+            arrived(other, 3, first)
+            arrived(other, 3, first + 2)
+            multiply(other, 3, first, 2)
         for copy in sent:
             copy.wait_send()
 
@@ -224,12 +230,12 @@
             copy.start()
             sent.append(copy)
 
-        for h in range(2):
+        for h in range(4):
             send(same, 1, h, to_out, layer=outward)
             send(same, 1, h, to_in, layer=inward)
             send(same, 1, h, to_x, row=1 - x)
             share_rows(1, h)
-        for h in range(2):
+        for h in range(4):
             arrived(same, 2, h)
             send(same, 2, h, to_out, layer=outward)
             send(same, 2, h, to_x, row=1 - x)
@@ -240,29 +246,32 @@
         base.wait()
         prepare(1)
         multiply(same, 1)
-        arrived(other, 1, 0)
-        arrived(other, 1, 1)
+        for h in range(4):
+            arrived(other, 1, h)
         multiply(other, 1)
-        for h in range(2):
+        for h in range(4):
             arrived(same, 3, h)
             send(same, 3, h, to_out, layer=outward)
+            share_rows(3, h)
+        for h in (2, 3, 0, 1):
             send(same, 3, h, to_x, row=1 - x)
-            share_rows(3, h)
         prepare(0)
         multiply(same, 0)
-        arrived(other, 0, 0)
-        arrived(other, 0, 1)
+        for h in range(4):
+            arrived(other, 0, h)
         multiply(other, 0)
         prepare(2)
         multiply(same, 2)
-        arrived(other, 2, 0)
-        arrived(other, 2, 1)
-        arrived(other, 3, 0)
-        arrived(other, 3, 1)
-        send(other, 3, 1, to_out, layer=outward)
+        for h in (2, 3):
+            arrived(other, 3, h)
+            send(other, 3, h, to_out, layer=outward)
+        for h in range(4):
+            arrived(other, 2, h)
         multiply(other, 2)
         prepare(3)
         multiply(same, 3)
+        for h in (0, 1):
+            arrived(other, 3, h)
         multiply(other, 3)
         for copy in sent:
             copy.wait_send()
@@ -270,14 +279,15 @@
     @pl.when(is_owner)
     def _():
         for k in range(4):
-            for h in range(2):
+            for h in range(4):
                 for copy in owner_copies(k, h):
                     copy.wait_send()
 
     @pl.when(is_far)
     def _():
         for k in range(4):
-            far_copy(k).wait_send()
+            for h in (lane, lane + 2):
+                far_copy(k, h).wait_send()
 
 
 def lined_up(panel, c_in):
@@ -294,13 +304,13 @@
             pltpu.VMEM((4, depth, narrow), jnp.float32),
             pltpu.VMEM((narrow, 3 * depth), jnp.bfloat16),
             dma, dma,
-            dma((2, 4, 2)),
-            dma((4, 2)),
-            dma((2, 4, 2)),
-            dma((2, 4, 2)),
-            dma((2, 4, 2)),
-            dma((4, 2)),
-            dma((4, 2)),
+            dma((2, 4, 4)),
+            dma((4, 4)),
+            dma((2, 4, 4)),
+            dma((2, 4, 4)),
+            dma((2, 4, 4)),
+            dma((4, 4)),
+            dma((4, 4)),
         ],
         compiler_params=pltpu.CompilerParams(
             collective_id=0, has_side_effects=True, vmem_limit_bytes=48 << 20

time: 94.3 us -> 92.4 us (0.980)
  Pallas kernels: 90.8 us -> 88.8 us
    pallas_call x1, Pallas kernels: 90.8 us -> 88.8 us  [lined_up(): pl.pallas_call(gather_and_update, out_shape=pltpu.VMEM((narrow, wide), jn...]
where the time goes in v2:
time: 92.4 us; the launch traced here: 92.2 us
  Pallas kernels  88.8 us (96%)
  local copies, waits for them, and re-layouts  3.4 us (4%)
    pallas_call x1, Pallas kernels, lined_up(): pl.pallas_call(gather_and_update, out_shape=pltpu.VMEM((narrow, wide), jn...  88.8 us
    unnamed x1, local copies, waits for them, and re-layouts  3.4 us

profile of v2, /device:TPU:0, one launch (start us, length us, event | category | flops | bytes accessed | tf_op | source)
XLA Modules:
  0.0 92.2 jit_solution(17913010563945740738)
XLA Ops:
  0.0 88.8 %shard_map.28 = f32[1024,2048]{1,0:T(8,128)S(1)} custom-call(f32[256,1024]{1,0:T(8,128)} %panel.1, f32[1024,2048]{1,0:T(8,128)} %bitcast.3), custom_call_target="tpu_custom_call" | custom-call | tf_op jit(solution)/shard_map/pallas_call | solution.py:297
  88.8 3.4 %copy.4 = f32[1,1,1024,2048]{3,2,1,0:T(8,128)} copy(f32[1,1,1024,2048]{3,2,1,0:T(8,128)S(1)} %bitcast.2) | data formatting | bytes 16777216
